TPU v7x, 32 devices: a whole 2x2x4 slice. The times are simulated.
32 devices in a mesh: grp: 16 (over z, x, core), fsdp: 2 (over y).
Axes of the slice: x: 2, y: 2, z: 4, core: 2. Of those that a mesh axis runs over, the one named last changes fastest.
Arguments:
- normalized_inputs: bfloat16 [4096, 2048], P(('grp', 'fsdp')), may hold values from -6 to 6
- output_sensitivity: bfloat16 [4096, 512], P(('grp', 'fsdp')), may hold values from -6 to 6
- projection_weights: bfloat16 [2048, 512], P('fsdp'), may hold values from -0.25 to 0.25
- completion_mask: int32 [16], replicated, may hold values 0 or 1
- replica_partition_list: int32 [16], replicated, may hold values from 0 to 3, as said below
Outputs:
- input_grad: bfloat16 [4096, 2048], P(('grp', 'fsdp'))
- weight_grad: float32 [2048, 512], P(('grp', 'fsdp'))
Inputs may be any that keep to these rules, and one draw needn't show every extreme that they name: `replica_partition_list`: each of the 4 block numbers is named by exactly 4 groups.
All inputs are finite; a program needn't handle non-finite values.
Results may differ from a plain program's by a relative error of at most 0.001.
Values may be sent and summed in bfloat16 or wider, within the bound.
A program may use at most 64 MiB of HBM per device.

v0:
```python
import jax
import jax.numpy as jnp
from jax import lax
from jax.sharding import PartitionSpec as P


def shards(
    normalized_inputs,
    output_sensitivity,
    projection_weights,
    completion_mask,
    replica_partition_list,
):
    replica_index = lax.axis_index("grp")
    selected_replica = lax.iota(jnp.int32, completion_mask.shape[0]) == replica_index
    assigned_piece = jnp.sum(jnp.where(selected_replica, replica_partition_list, 0))
    finished_indicator = jnp.sum(jnp.where(selected_replica, completion_mask, 0))
    finisher_tally = jnp.sum(
        jnp.where(replica_partition_list == assigned_piece, completion_mask, 0)
    )
    living_float = finished_indicator.astype(jnp.float32)
    decode_sum = living_float / (finisher_tally.astype(jnp.float32) + 1.0 - living_float)
    tokens_here = normalized_inputs.shape[0]
    model_width = normalized_inputs.shape[1]
    inner_size = lax.axis_size("fsdp")
    outer_size = lax.axis_size("grp")
    input_grad = lax.dot_general(
        output_sensitivity,
        lax.all_gather(projection_weights, "fsdp", axis=0, tiled=True),
        (((1,), (1,)), ((), ())),
        preferred_element_type=jnp.float32,
    ).astype(jnp.bfloat16)
    owner_rows = model_width // (outer_size * inner_size)
    reordered = normalized_inputs.reshape(tokens_here, outer_size, inner_size, owner_rows)
    reordered = reordered.transpose(0, 2, 1, 3).reshape(tokens_here, model_width)
    column_block = lax.all_to_all(reordered, "fsdp", split_axis=1, concat_axis=0, tiled=True)
    group_block = lax.dot_general(
        column_block,
        lax.all_gather(output_sensitivity, "fsdp", axis=0, tiled=True),
        (((0,), (0,)), ((), ())),
        preferred_element_type=jnp.float32,
    )
    weight_grad = lax.psum_scatter(decode_sum * group_block, "grp", scatter_dimension=0, tiled=True)
    return (input_grad, weight_grad)


def solution(mesh):
    in_specs = (P(("grp", "fsdp"), None), P(("grp", "fsdp"), None), P("fsdp", None), P(), P())
    out_specs = (P(("grp", "fsdp"), None), P(("grp", "fsdp"), None))
    return jax.shard_map(shards, mesh=mesh, in_specs=in_specs, out_specs=out_specs, check_vma=False)
```

profile of v0, /device:TPU:0, one launch (start us, length us, event | category | flops | bytes accessed | tf_op | source)
XLA Modules:
  0.0 103.5 jit_solution(11844051414717168512)
XLA Ops:
  8.0 0.0 copy-start.2
  8.0 0.0 copy-start.1
  8.0 0.0 copy-start
  8.0 0.0 all-gather.2.cloned.1.call-start
  8.1 0.7 all-gather.2.cloned.1.call-update
  8.8 1.3 %copy.7 = bf16[128,2048]{0,1:T(8,128)(2,1)S(1)} copy(bf16[128,2048]{1,0:T(8,128)(2,1)} %param.5) | data formatting | bytes 1048576 | tf_op args[0]
  10.1 0.8 copy.8
  10.9 4.3 %all-to-all-start = ((bf16[128,2,1024]{0,2,1:T(8,128)(2,1)}), bf16[128,2,1024]{0,2,1:T(8,128)(2,1)S(1)}, u32[]{:S(2)}, u32[]{:S(2)}) async-start(bf16[128,2,1024]{0,2,1:T(8,128)(2,1)} %bitcast.2), calls=%async_computation | async-start | bytes 1048576 | tf_op jit(solution)/shard_map/all_to_all | solution.py:36
  15.2 0.0 reduce-scatter.2.cloned.1.call-start
  15.2 0.0 copy-done.2
  15.2 0.6 fusion.1
  15.8 0.0 copy-done.1
  15.8 1.3 %fusion.2 = (s32[]{:T(128)}, s32[]{:T(128)}) fusion(s32[16]{0:T(128)S(1)} %copy-done.1, s32[16]{0:T(128)S(1)} %copy-done.2, s32[]{:T(128)} %fusion.1, s32[]{:T(128)S(6)} %axis_index.15), kind=kLoop, calls=%fused_computation.7 | loop fusion | flops 94 | bytes 144 | tf_op jit(solution)/shard_map/reduce_sum | solution.py:18
  18.4 0.0 copy-done
  18.4 12.3 %all_gather.7 = bf16[256,512]{1,0:T(8,128)(2,1)S(1)} all-gather(bf16[128,512]{1,0:T(8,128)(2,1)S(1)} %copy-done), channel_id=1, replica_groups=mesh['grp'=16,'fsdp'=2] {'fsdp'}, dimensions={0}, use_global_device_ids=true | all-gather | bytes 393216 | tf_op jit(solution)/shard_map/all_gather | solution.py:39
  30.7 0.0 all-to-all-done
  30.7 0.2 copy.9
  30.9 1.8 %convolution_multiply_fusion = f32[1024,512]{1,0:T(8,128)} fusion(bf16[256,1024]{1,0:T(8,128)(2,1)S(1)} %bitcast.12, bf16[256,512]{1,0:T(8,128)(2,1)S(1)} %all_gather.7, f32[]{:T(128)S(6)} %div.3), kind=kOutput, calls=%fused_computation.1 | convolution fusion | flops 268959744 | bytes 2883588 | tf_op jit(solution)/shard_map/dot_general | solution.py:37
  32.7 0.0 reduce-scatter.2.cloned.1.call-update
  32.7 16.7 %all-gather.2.cloned.1.call-done = bf16[2048,512]{1,0:T(8,128)(2,1)} async-done(((bf16[1024,512]{1,0:T(8,128)(2,1)}), bf16[2048,512]{1,0:T(8,128)(2,1)}) %all-gather.2.cloned.1.call-update) | async-done | bytes 2097168 | tf_op jit(solution)/shard_map/all_gather | solution.py:29
  49.4 3.2 %convolution_convert_fusion = bf16[128,2048]{1,0:T(8,128)(2,1)} fusion(bf16[128,512]{1,0:T(8,128)(2,1)S(1)} %copy-done, bf16[2048,512]{1,0:T(8,128)(2,1)} %all-gather.2.cloned.1.call-done), kind=kOutput, calls=%fused_computation | convolution fusion | flops 268697600 | bytes 2752512 | tf_op jit(solution)/shard_map/dot_general | solution.py:27
  52.7 43.4 %reduce-scatter.2.cloned.1.call-done = f32[64,512]{1,0:T(8,128)} async-done(((f32[1024,512]{1,0:T(8,128)}), f32[64,512]{1,0:T(8,128)}) %reduce-scatter.2.cloned.1.call-update) | async-done | bytes 131088 | tf_op jit(solution)/shard_map/reduce_scatter | solution.py:43
Async XLA Ops:
  8.0 7.2 %copy-start.2 = (s32[16]{0:T(128)S(1)}, s32[16]{0:T(128)}, u32[]{:S(2)}) copy-start(s32[16]{0:T(128)} %param.9) | copy-start | bytes 196
  8.0 7.8 %copy-start.1 = (s32[16]{0:T(128)S(1)}, s32[16]{0:T(128)}, u32[]{:S(2)}) copy-start(s32[16]{0:T(128)} %param.8) | copy-start | bytes 196
  8.0 10.4 %copy-start = (bf16[128,512]{1,0:T(8,128)(2,1)S(1)}, bf16[128,512]{1,0:T(8,128)(2,1)}, u32[]{:S(2)}) copy-start(bf16[128,512]{1,0:T(8,128)(2,1)} %param.6) | copy-start | bytes 393220
  8.0 41.4 %all-gather.2.cloned.1.call-start = ((), (), s32[]{:S(2)}) async-start(), calls=%async_computation.2 | async-start | bytes 3145728 | tf_op jit(solution)/shard_map/all_gather | solution.py:29
  10.9 19.8 %all-to-all-start = ((bf16[128,2,1024]{0,2,1:T(8,128)(2,1)}), bf16[128,2,1024]{0,2,1:T(8,128)(2,1)S(1)}, u32[]{:S(2)}, u32[]{:S(2)}) async-start(bf16[128,2,1024]{0,2,1:T(8,128)(2,1)} %bitcast.2), calls=%async_computation | async-start | bytes 1048576 | tf_op jit(solution)/shard_map/all_to_all | solution.py:36
  15.2 80.9 %reduce-scatter.2.cloned.1.call-start = ((), (), s32[]{:S(2)}) async-start(), calls=%async_computation.3 | async-start | bytes 2228224 | tf_op jit(solution)/shard_map/reduce_scatter | solution.py:43
Sparse Core Ops, SparseCore 0:
  10.4 39.0 all-gather.1
Sparse Core Ops, SparseCore 1:
  32.8 63.2 reduce-scatter.1
where the time goes:
time: 104 us
  waiting for transfers between devices  60.8 us (58%)
  between operations  16.8 us (16%)
  blocking collectives  12.3 us (12%)
  matrix products  5.03 us (5%)
  starting transfers between devices  4.3 us (4%)
  local copies, waits for them, and re-layouts  2.37 us (2%)
  other arithmetic  1.94 us (2%)
    reduce_scatter x1, waiting for transfers between devices, shards(): lax.psum_scatter(decode_sum * group_block, 'grp', scatter_dimension=0, ti...  43.4 us
    all_gather x1, waiting for transfers between devices, shards(): lax.all_gather(projection_weights, 'fsdp', axis=0, tiled=True)  16.7 us
    all_gather x1, blocking collectives, shards(): lax.all_gather(output_sensitivity, 'fsdp', axis=0, tiled=True)  12.3 us
    all_to_all x1, starting transfers between devices, shards(): lax.all_to_all(reordered, 'fsdp', split_axis=1, concat_axis=0, tiled=True)  4.26 us
    dot_general x1, matrix products, shards(): lax.dot_general(output_sensitivity, lax.all_gather(projection_weights, 'f...  3.25 us
  transfers between devices with their start and end apart: 3, of which 2 were waited for; matrix products, arithmetic and copies ran while one was open for 9% of the time, Pallas kernels for 0%

commit v1 on v0

--- a/solution.py
+++ b/solution.py
@@ -1,10 +1,18 @@
+import functools
+
 import jax
 import jax.numpy as jnp
 from jax import lax
+from jax.experimental import pallas as pl
+from jax.experimental.pallas import tpu as pltpu
 from jax.sharding import PartitionSpec as P
 
-
-def shards(
+MESH = pl.DeviceIdType.MESH
+CORES = 2
+WIDE = 2
+
+
+def collective_shards(
     normalized_inputs,
     output_sensitivity,
     projection_weights,
@@ -44,7 +52,239 @@
     return (input_grad, weight_grad)
 
 
+def kernel(
+    deep,
+    mask_ref, list_ref, x_hbm, s_hbm, w_hbm,
+    ig_hbm, wg_ref,
+    x_v, s_v, w_v, tx, rx, px_send, px_recv, q, zr, ig_own, ig_send, ig_recv,
+    load_sem, out_sem, s_send_sem, s_recv_sem, x_send_sem, x_recv_sem,
+    px_send_sem, px_recv_sem, z_send_sem, z_recv_sem, ig_send_sem, ig_recv_sem,
+):
+    grp = lax.axis_index("grp")
+    y = lax.axis_index("fsdp")
+    core = lax.rem(grp, CORES)
+    wide = lax.rem(grp // CORES, WIDE)
+    z = grp // (CORES * WIDE)
+    oy, oc = 1 - y, 1 - core
+    tokens = s_hbm.shape[0]
+    groups = mask_ref.shape[0]
+    rows = wg_ref.shape[0]
+    half = w_hbm.shape[0]
+
+    def at(zz, xx, cc, yy):
+        return ((zz * WIDE + xx) * CORES + cc, yy)
+
+    def remote(src, dst, send, recv, device):
+        copy = pltpu.make_async_remote_copy(
+            src_ref=src, dst_ref=dst, send_sem=send, recv_sem=recv,
+            device_id=device, device_id_type=MESH,
+        )
+        return copy
+
+    y_peer = at(z, wide, core, oy)
+    y_cross = at(z, wide, oc, oy)
+    sibling = at(z, wide, oc, y)
+    x_peer = at(z, 1 - wide, core, y)
+    z_to = [at(lax.rem(z + k, deep), wide, core, y) for k in range(1, deep)]
+    me = core * 2 + y
+    from_y = core * 2 + oy
+    from_cross = oc * 2 + oy
+    from_sib = oc * 2 + y
+
+    load_s = pltpu.make_async_copy(s_hbm, s_v.at[me], load_sem.at[0])
+    load_x = pltpu.make_async_copy(x_hbm, x_v, load_sem.at[1])
+    load_w = pltpu.make_async_copy(w_hbm, w_v, load_sem.at[2])
+    load_s.start()
+    load_x.start()
+    load_w.start()
+
+    barrier = pltpu.get_barrier_semaphore()
+    partners = [y_peer, y_cross, sibling, x_peer] + z_to
+    for partner in partners:
+        pl.semaphore_signal(barrier, inc=1, device_id=partner, device_id_type=MESH)
+
+    order = [k for k in range(1, deep)] + [0]
+    span = WIDE * CORES * 2 * rows
+
+    def turn(k):
+        zz = lax.rem(z + k, deep)
+        part = x_v[:, pl.ds(pl.multiple_of(zz * span, span), span)].T
+        for xx in range(WIDE):
+            for cy in range(CORES * 2):
+                start = (xx * CORES * 2 + cy) * rows
+                tx[k, cy, xx * rows:(xx + 1) * rows, :] = part[start:start + rows, :]
+
+    load_x.wait()
+    turn(order[0])
+    load_s.wait()
+    pl.semaphore_wait(barrier, len(partners))
+
+    s_y = remote(s_v.at[me], s_v.at[me], s_send_sem.at[0], s_recv_sem.at[0], y_peer)
+    s_sib = remote(s_v.at[me], s_v.at[me], s_send_sem.at[1], s_recv_sem.at[1], sibling)
+    s_fwd = remote(s_v.at[from_y], s_v.at[from_y], s_send_sem.at[2], s_recv_sem.at[2], sibling)
+    s_y.start()
+    s_sib.start()
+
+    x_copies = {}
+    for n, k in enumerate(order):
+        if n:
+            turn(k)
+        copies = []
+        for slot, (device, there) in enumerate(
+            ((y_peer, from_y), (y_cross, from_cross), (sibling, from_sib))
+        ):
+            copy = remote(
+                tx.at[k, there], rx.at[k, me], x_send_sem.at[k, slot], x_recv_sem.at[k, slot], device
+            )
+            copy.start()
+            copies.append(copy)
+        x_copies[k] = copies
+        rx[k, me] = tx[k, me]
+
+    scales = []
+    for cc in range(CORES):
+        here = (z * WIDE + wide) * CORES + cc
+        mine = list_ref[here]
+        tally = jnp.int32(0)
+        for h in range(groups):
+            tally = tally + jnp.where(list_ref[h] == mine, mask_ref[h], 0)
+        done = jnp.full((1, wg_ref.shape[1]), mask_ref[here], jnp.int32).astype(jnp.float32)
+        total = jnp.full((1, wg_ref.shape[1]), tally, jnp.int32).astype(jnp.float32)
+        scales.append(done / (total + 1.0 - done))
+
+    load_w.wait()
+
+    def grad(s_block):
+        return lax.dot_general(
+            s_block, w_v[...], (((1,), (1,)), ((), ())), preferred_element_type=jnp.float32
+        ).astype(jnp.bfloat16)
+
+    own_columns = pl.ds(pl.multiple_of(y * half, half), half)
+    other_columns = pl.ds(pl.multiple_of(oy * half, half), half)
+    ig_own[...] = grad(s_v[me])
+    own_out = pltpu.make_async_copy(ig_own, ig_hbm.at[:, own_columns], out_sem.at[0])
+    own_out.start()
+
+    s_y.wait_recv()
+    s_fwd.start()
+    ig_send[...] = grad(s_v[from_y])
+    ig_copy = remote(ig_send, ig_recv, ig_send_sem, ig_recv_sem, y_peer)
+    ig_copy.start()
+
+    s_sib.wait_recv()
+    s_fwd.wait_recv()
+
+    px_copies, z_copies = {}, {}
+
+    def partial(k):
+        for copy in x_copies[k]:
+            copy.wait_recv()
+        total = None
+        for cc in range(CORES):
+            left = jnp.concatenate([rx[k, cc * 2], rx[k, cc * 2 + 1]], axis=1)
+            right = s_v[cc * 2:cc * 2 + 2].reshape(2 * tokens, s_v.shape[2])
+            product = scales[cc] * jnp.dot(left, right, preferred_element_type=jnp.float32)
+            total = product if total is None else total + product
+        for xx in range(WIDE):
+            q_or_send[xx](k, total[xx * rows:(xx + 1) * rows])
+
+    def put0(k, value):
+        both[k, 0] = value
+
+    def put1(k, value):
+        both[k, 1] = value
+
+    both = px_send
+    q_or_send = (put0, put1)
+
+    def send_x(k):
+        copy = remote(
+            px_send.at[k, 1 - wide], px_recv.at[k], px_send_sem.at[k], px_recv_sem.at[k], x_peer
+        )
+        copy.start()
+        px_copies[k] = copy
+
+    def gather_x(k):
+        px_copies[k].wait_recv()
+        q[k] = px_send[k, wide] + px_recv[k]
+        if k:
+            copy = remote(q.at[k], zr.at[k], z_send_sem.at[k], z_recv_sem.at[k], z_to[k - 1])
+            copy.start()
+            z_copies[k] = copy
+
+    for n, k in enumerate(order):
+        partial(k)
+        send_x(k)
+        if n:
+            gather_x(order[n - 1])
+    gather_x(order[-1])
+
+    total = q[0]
+    for k in range(1, deep):
+        z_copies[k].wait_recv()
+        total = total + zr[k]
+    wg_ref[...] = total
+
+    ig_copy.wait_recv()
+    other_out = pltpu.make_async_copy(ig_recv, ig_hbm.at[:, other_columns], out_sem.at[1])
+    other_out.start()
+
+    for copy in (s_y, s_sib, s_fwd, ig_copy):
+        copy.wait_send()
+    for copies in x_copies.values():
+        for copy in copies:
+            copy.wait_send()
+    for copy in list(px_copies.values()) + list(z_copies.values()):
+        copy.wait_send()
+    own_out.wait()
+    other_out.wait()
+
+
+def kernel_shards(deep, rows, x, s, w, mask, plist):
+    tokens, width = x.shape
+    values = s.shape[1]
+    f32, bf16 = jnp.float32, jnp.bfloat16
+    dma = pltpu.SemaphoreType.DMA
+    anywhere = pl.BlockSpec(memory_space=pl.ANY)
+    smem = pl.BlockSpec(memory_space=pltpu.SMEM)
+    wide_rows = WIDE * rows
+    return pl.pallas_call(
+        functools.partial(kernel, deep),
+        out_shape=(
+            jax.ShapeDtypeStruct((tokens, width), bf16),
+            jax.ShapeDtypeStruct((rows, values), f32),
+        ),
+        in_specs=[smem, smem, anywhere, anywhere, anywhere],
+        out_specs=(anywhere, pl.BlockSpec(memory_space=pltpu.VMEM)),
+        scratch_shapes=[
+            pltpu.VMEM((tokens, width), bf16),
+            pltpu.VMEM((CORES * 2, tokens, values), bf16),
+            pltpu.VMEM(w.shape, bf16),
+            pltpu.VMEM((deep, CORES * 2, wide_rows, tokens), bf16),
+            pltpu.VMEM((deep, CORES * 2, wide_rows, tokens), bf16),
+            pltpu.VMEM((deep, WIDE, rows, values), f32),
+            pltpu.VMEM((deep, rows, values), f32),
+            pltpu.VMEM((deep, rows, values), f32),
+            pltpu.VMEM((deep, rows, values), f32),
+            pltpu.VMEM((tokens, w.shape[0]), bf16),
+            pltpu.VMEM((tokens, w.shape[0]), bf16),
+            pltpu.VMEM((tokens, w.shape[0]), bf16),
+            dma((3,)), dma((2,)), dma((3,)), dma((3,)), dma((deep, 3)), dma((deep, 3)),
+            dma((deep,)), dma((deep,)), dma((deep,)), dma((deep,)), dma, dma,
+        ],
+        compiler_params=pltpu.CompilerParams(collective_id=0, has_side_effects=True),
+    )(mask, plist, x, s, w)
+
+
 def solution(mesh):
+    outer, inner = mesh.shape["grp"], mesh.shape["fsdp"]
+
+    def shards(x, s, w, mask, plist):
+        rows = x.shape[1] // (outer * inner)
+        if inner == 2 and outer % (CORES * WIDE) == 0 and rows % 16 == 0 and x.shape[0] % 128 == 0:
+            return tuple(kernel_shards(outer // (CORES * WIDE), rows, x, s, w, mask, plist))
+        return collective_shards(x, s, w, mask, plist)
+
     in_specs = (P(("grp", "fsdp"), None), P(("grp", "fsdp"), None), P("fsdp", None), P(), P())
     out_specs = (P(("grp", "fsdp"), None), P(("grp", "fsdp"), None))
     return jax.shard_map(shards, mesh=mesh, in_specs=in_specs, out_specs=out_specs, check_vma=False)

time: 104 us -> 36.5 us (0.35)
  waiting for transfers between devices: 60.8 us -> 0 us
  Pallas kernels: 0 us -> 33.1 us
  between operations: 16.8 us -> 0.65 us
  blocking collectives: 12.3 us -> 0 us
  matrix products: 5.03 us -> 0 us
  starting transfers between devices: 4.3 us -> 0 us
  other arithmetic: 1.94 us -> 0 us
    reduce_scatter x1 -> x0, waiting for transfers between devices: 43.4 us -> none  [shards(): lax.psum_scatter(decode_sum * group_block, 'grp', scatter_dimension=0, ti...]
    pallas_call x0 -> x1, Pallas kernels: none -> 33.1 us  [kernel_shards(): pl.pallas_call(functools.partial(kernel, deep), out_shape=(jax.ShapeDtype...]
    all_gather x1 -> x0, waiting for transfers between devices: 16.7 us -> none  [shards(): lax.all_gather(projection_weights, 'fsdp', axis=0, tiled=True)]
    all_gather x1 -> x0, blocking collectives: 12.3 us -> none  [shards(): lax.all_gather(output_sensitivity, 'fsdp', axis=0, tiled=True)]
    dot_general x2 -> x0, matrix products: 5.03 us -> none  [the longest x1 3.25 us: shards(): lax.dot_general(output_sensitivity, lax.all_gather(projection_weights, 'f...]
    all_to_all x1 -> x0, starting transfers between devices: 4.26 us -> none  [shards(): lax.all_to_all(reordered, 'fsdp', split_axis=1, concat_axis=0, tiled=True)]
    reduce_sum x2 -> x0, other arithmetic: 1.94 us -> none  [the longest x1 1.31 us: shards(): jnp.sum(jnp.where(replica_partition_list == assigned_piece, completion_ma...]
    unnamed x7 -> x4, local copies, waits for them, and re-layouts: 1.32 us -> 2.58 us
  transfers between devices with their start and end apart: 3 -> 0, of which waited for: 2 -> 0; matrix products, arithmetic and copies ran while one was open for 9% -> 0% of each run, Pallas kernels for 0% -> 0%
where the time goes in v1:
time: 36.5 us; the launch traced here: 36.4 us
  Pallas kernels  33.1 us (91%)
  local copies, waits for them, and re-layouts  2.58 us (7%)
  between operations  0.65 us (2%)
    pallas_call x1, Pallas kernels, kernel_shards(): pl.pallas_call(functools.partial(kernel, deep), out_shape=(jax.ShapeDtype...  33.1 us
    unnamed x4, local copies, waits for them, and re-layouts  2.58 us

profile of v1, /device:TPU:0, one launch (start us, length us, event | category | flops | bytes accessed | tf_op | source)
XLA Modules:
  0.0 36.4 jit_solution(13793980970731114408)
XLA Ops:
  0.6 33.1 %shard_map.68 = (bf16[128,2048]{1,0:T(8,128)(2,1)}, f32[64,512]{1,0:T(8,128)}) custom-call(s32[16]{0:T(128)} %mask_ref.1, s32[16]{0:T(128)} %list_ref.1, bf16[128,2048]{1,0:T(8,128)(2,1)} %x_hbm.1, bf16[128,512]{1,0:T(8,128)(2,1)} %s_hbm.1, bf16[1024,512]{1,0:T(8,128)(2,1)} %w_hbm.1), custom_call_target="tpu_custom_call" | custom-call | tf_op jit(solution)/shard_map/pallas_call | solution.py:251
  33.8 0.0 copy-start
  33.8 1.9 %copy.9 = bf16[128,2048]{1,0:T(8,128)(2,1)} copy(bf16[128,2048]{1,0:T(8,128)(2,1)} %get-tuple-element.4) | data formatting | bytes 1048576
  35.7 0.0 copy-done
  35.7 0.7 %copy.10 = f32[64,512]{1,0:T(8,128)} copy(f32[64,512]{1,0:T(8,128)S(1)} %copy-done) | data formatting | bytes 262144
Async XLA Ops:
  33.8 1.9 %copy-start = (f32[64,512]{1,0:T(8,128)S(1)}, f32[64,512]{1,0:T(8,128)}, u32[]{:S(2)}) copy-start(f32[64,512]{1,0:T(8,128)} %get-tuple-element.5) | copy-start | bytes 393220

commit v2 on v1

--- a/solution.py
+++ b/solution.py
@@ -10,6 +10,8 @@
 MESH = pl.DeviceIdType.MESH
 CORES = 2
 WIDE = 2
+STEPS = 32766.0
+TINY = 1e-33
 
 
 def collective_shards(
@@ -52,11 +54,22 @@
     return (input_grad, weight_grad)
 
 
+def encode(value):
+    top = jnp.maximum(jnp.max(jnp.abs(value), axis=0, keepdims=True), TINY)
+    coded = jnp.round(value * (STEPS / top)).astype(jnp.int32).astype(jnp.int16)
+    return coded, top * (1.0 / STEPS)
+
+
+def decoded(coded, step):
+    return coded.astype(jnp.int32).astype(jnp.float32) * step
+
+
 def kernel(
     deep,
     mask_ref, list_ref, x_hbm, s_hbm, w_hbm,
     ig_hbm, wg_ref,
-    x_v, s_v, w_v, tx, rx, px_send, px_recv, q, zr, ig_own, ig_send, ig_recv,
+    x_v, s_v, w_v, tx, rx, own_part, px_send, px_scale, px_recv, px_rscale,
+    q, q_send, q_scale, zr, zr_scale, ig_own, ig_send, ig_recv,
     load_sem, out_sem, s_send_sem, s_recv_sem, x_send_sem, x_recv_sem,
     px_send_sem, px_recv_sem, z_send_sem, z_recv_sem, ig_send_sem, ig_recv_sem,
 ):
@@ -185,32 +198,38 @@
             right = s_v[cc * 2:cc * 2 + 2].reshape(2 * tokens, s_v.shape[2])
             product = scales[cc] * jnp.dot(left, right, preferred_element_type=jnp.float32)
             total = product if total is None else total + product
-        for xx in range(WIDE):
-            q_or_send[xx](k, total[xx * rows:(xx + 1) * rows])
-
-    def put0(k, value):
-        both[k, 0] = value
-
-    def put1(k, value):
-        both[k, 1] = value
-
-    both = px_send
-    q_or_send = (put0, put1)
+        own_part[k, 0] = total[:rows]
+        own_part[k, 1] = total[rows:]
+        coded, scale = encode(own_part[k, 1 - wide])
+        px_send[k] = coded
+        px_scale[k] = scale
 
     def send_x(k):
-        copy = remote(
-            px_send.at[k, 1 - wide], px_recv.at[k], px_send_sem.at[k], px_recv_sem.at[k], x_peer
-        )
-        copy.start()
-        px_copies[k] = copy
+        copies = [
+            remote(px_send.at[k], px_recv.at[k], px_send_sem.at[k, 0], px_recv_sem.at[k, 0], x_peer),
+            remote(px_scale.at[k], px_rscale.at[k], px_send_sem.at[k, 1], px_recv_sem.at[k, 1], x_peer),
+        ]
+        for copy in copies:
+            copy.start()
+        px_copies[k] = copies
 
     def gather_x(k):
-        px_copies[k].wait_recv()
-        q[k] = px_send[k, wide] + px_recv[k]
+        for copy in px_copies[k]:
+            copy.wait_recv()
+        value = own_part[k, wide] + decoded(px_recv[k], px_rscale[k])
         if k:
-            copy = remote(q.at[k], zr.at[k], z_send_sem.at[k], z_recv_sem.at[k], z_to[k - 1])
-            copy.start()
-            z_copies[k] = copy
+            coded, scale = encode(value)
+            q_send[k] = coded
+            q_scale[k] = scale
+            copies = [
+                remote(q_send.at[k], zr.at[k], z_send_sem.at[k, 0], z_recv_sem.at[k, 0], z_to[k - 1]),
+                remote(q_scale.at[k], zr_scale.at[k], z_send_sem.at[k, 1], z_recv_sem.at[k, 1], z_to[k - 1]),
+            ]
+            for copy in copies:
+                copy.start()
+            z_copies[k] = copies
+        else:
+            q[...] = value
 
     for n, k in enumerate(order):
         partial(k)
@@ -219,10 +238,11 @@
             gather_x(order[n - 1])
     gather_x(order[-1])
 
-    total = q[0]
+    total = q[...]
     for k in range(1, deep):
-        z_copies[k].wait_recv()
-        total = total + zr[k]
+        for copy in z_copies[k]:
+            copy.wait_recv()
+        total = total + decoded(zr[k], zr_scale[k])
     wg_ref[...] = total
 
     ig_copy.wait_recv()
@@ -231,11 +251,10 @@
 
     for copy in (s_y, s_sib, s_fwd, ig_copy):
         copy.wait_send()
-    for copies in x_copies.values():
-        for copy in copies:
-            copy.wait_send()
-    for copy in list(px_copies.values()) + list(z_copies.values()):
-        copy.wait_send()
+    for group in (x_copies, px_copies, z_copies):
+        for copies in group.values():
+            for copy in copies:
+                copy.wait_send()
     own_out.wait()
     other_out.wait()
 
@@ -243,7 +262,7 @@
 def kernel_shards(deep, rows, x, s, w, mask, plist):
     tokens, width = x.shape
     values = s.shape[1]
-    f32, bf16 = jnp.float32, jnp.bfloat16
+    f32, bf16, i16 = jnp.float32, jnp.bfloat16, jnp.int16
     dma = pltpu.SemaphoreType.DMA
     anywhere = pl.BlockSpec(memory_space=pl.ANY)
     smem = pl.BlockSpec(memory_space=pltpu.SMEM)
@@ -263,14 +282,20 @@
             pltpu.VMEM((deep, CORES * 2, wide_rows, tokens), bf16),
             pltpu.VMEM((deep, CORES * 2, wide_rows, tokens), bf16),
             pltpu.VMEM((deep, WIDE, rows, values), f32),
-            pltpu.VMEM((deep, rows, values), f32),
-            pltpu.VMEM((deep, rows, values), f32),
-            pltpu.VMEM((deep, rows, values), f32),
+            pltpu.VMEM((deep, rows, values), i16),
+            pltpu.VMEM((deep, 1, values), f32),
+            pltpu.VMEM((deep, rows, values), i16),
+            pltpu.VMEM((deep, 1, values), f32),
+            pltpu.VMEM((rows, values), f32),
+            pltpu.VMEM((deep, rows, values), i16),
+            pltpu.VMEM((deep, 1, values), f32),
+            pltpu.VMEM((deep, rows, values), i16),
+            pltpu.VMEM((deep, 1, values), f32),
             pltpu.VMEM((tokens, w.shape[0]), bf16),
             pltpu.VMEM((tokens, w.shape[0]), bf16),
             pltpu.VMEM((tokens, w.shape[0]), bf16),
             dma((3,)), dma((2,)), dma((3,)), dma((3,)), dma((deep, 3)), dma((deep, 3)),
-            dma((deep,)), dma((deep,)), dma((deep,)), dma((deep,)), dma, dma,
+            dma((deep, 2)), dma((deep, 2)), dma((deep, 2)), dma((deep, 2)), dma, dma,
         ],
         compiler_params=pltpu.CompilerParams(collective_id=0, has_side_effects=True),
     )(mask, plist, x, s, w)

time: 36.5 us -> 29.8 us (0.82)
  Pallas kernels: 33.1 us -> 26.4 us
    pallas_call x1, Pallas kernels: 33.1 us -> 26.4 us  [kernel_shards(): pl.pallas_call(functools.partial(kernel, deep), out_shape=(jax.ShapeDtype...]
where the time goes in v2:
time: 29.8 us; the launch traced here: 29.7 us
  Pallas kernels  26.4 us (89%)
  local copies, waits for them, and re-layouts  2.58 us (9%)
  between operations  0.65 us (2%)
    pallas_call x1, Pallas kernels, kernel_shards(): pl.pallas_call(functools.partial(kernel, deep), out_shape=(jax.ShapeDtype...  26.4 us
    unnamed x4, local copies, waits for them, and re-layouts  2.58 us

profile of v2, /device:TPU:0, one launch (start us, length us, event | category | flops | bytes accessed | tf_op | source)
XLA Modules:
  0.0 29.7 jit_solution(9588256946594312013)
XLA Ops:
  0.6 26.4 %shard_map.68 = (bf16[128,2048]{1,0:T(8,128)(2,1)}, f32[64,512]{1,0:T(8,128)}) custom-call(s32[16]{0:T(128)} %mask_ref.1, s32[16]{0:T(128)} %list_ref.1, bf16[128,2048]{1,0:T(8,128)(2,1)} %x_hbm.1, bf16[128,512]{1,0:T(8,128)(2,1)} %s_hbm.1, bf16[1024,512]{1,0:T(8,128)(2,1)} %w_hbm.1), custom_call_target="tpu_custom_call" | custom-call | tf_op jit(solution)/shard_map/pallas_call | solution.py:270
  27.1 0.0 copy-start
  27.1 1.9 %copy.9 = bf16[128,2048]{1,0:T(8,128)(2,1)} copy(bf16[128,2048]{1,0:T(8,128)(2,1)} %get-tuple-element.4) | data formatting | bytes 1048576
  29.0 0.0 copy-done
  29.0 0.7 %copy.10 = f32[64,512]{1,0:T(8,128)} copy(f32[64,512]{1,0:T(8,128)S(1)} %copy-done) | data formatting | bytes 262144
Async XLA Ops:
  27.1 1.9 %copy-start = (f32[64,512]{1,0:T(8,128)S(1)}, f32[64,512]{1,0:T(8,128)}, u32[]{:S(2)}) copy-start(f32[64,512]{1,0:T(8,128)} %get-tuple-element.5) | copy-start | bytes 393220

commit v3 on v2

--- a/solution.py
+++ b/solution.py
@@ -67,10 +67,10 @@
 def kernel(
     deep,
     mask_ref, list_ref, x_hbm, s_hbm, w_hbm,
-    ig_hbm, wg_ref,
+    ig_ref, wg_ref,
     x_v, s_v, w_v, tx, rx, own_part, px_send, px_scale, px_recv, px_rscale,
-    q, q_send, q_scale, zr, zr_scale, ig_own, ig_send, ig_recv,
-    load_sem, out_sem, s_send_sem, s_recv_sem, x_send_sem, x_recv_sem,
+    q, q_send, q_scale, zr, zr_scale, ig_send,
+    load_sem, s_send_sem, s_recv_sem, x_send_sem, x_recv_sem,
     px_send_sem, px_recv_sem, z_send_sem, z_recv_sem, ig_send_sem, ig_recv_sem,
 ):
     grp = lax.axis_index("grp")
@@ -173,15 +173,12 @@
         ).astype(jnp.bfloat16)
 
     own_columns = pl.ds(pl.multiple_of(y * half, half), half)
-    other_columns = pl.ds(pl.multiple_of(oy * half, half), half)
-    ig_own[...] = grad(s_v[me])
-    own_out = pltpu.make_async_copy(ig_own, ig_hbm.at[:, own_columns], out_sem.at[0])
-    own_out.start()
+    ig_ref[:, own_columns] = grad(s_v[me])
 
     s_y.wait_recv()
     s_fwd.start()
     ig_send[...] = grad(s_v[from_y])
-    ig_copy = remote(ig_send, ig_recv, ig_send_sem, ig_recv_sem, y_peer)
+    ig_copy = remote(ig_send, ig_ref.at[:, own_columns], ig_send_sem, ig_recv_sem, y_peer)
     ig_copy.start()
 
     s_sib.wait_recv()
@@ -246,8 +243,6 @@
     wg_ref[...] = total
 
     ig_copy.wait_recv()
-    other_out = pltpu.make_async_copy(ig_recv, ig_hbm.at[:, other_columns], out_sem.at[1])
-    other_out.start()
 
     for copy in (s_y, s_sib, s_fwd, ig_copy):
         copy.wait_send()
@@ -255,8 +250,6 @@
         for copies in group.values():
             for copy in copies:
                 copy.wait_send()
-    own_out.wait()
-    other_out.wait()
 
 
 def kernel_shards(deep, rows, x, s, w, mask, plist):
@@ -270,11 +263,11 @@
     return pl.pallas_call(
         functools.partial(kernel, deep),
         out_shape=(
-            jax.ShapeDtypeStruct((tokens, width), bf16),
-            jax.ShapeDtypeStruct((rows, values), f32),
+            pltpu.VMEM((tokens, width), bf16),
+            pltpu.VMEM((rows, values), f32),
         ),
         in_specs=[smem, smem, anywhere, anywhere, anywhere],
-        out_specs=(anywhere, pl.BlockSpec(memory_space=pltpu.VMEM)),
+        out_specs=(pl.BlockSpec(memory_space=pltpu.VMEM),) * 2,
         scratch_shapes=[
             pltpu.VMEM((tokens, width), bf16),
             pltpu.VMEM((CORES * 2, tokens, values), bf16),
@@ -292,9 +285,7 @@
             pltpu.VMEM((deep, rows, values), i16),
             pltpu.VMEM((deep, 1, values), f32),
             pltpu.VMEM((tokens, w.shape[0]), bf16),
-            pltpu.VMEM((tokens, w.shape[0]), bf16),
-            pltpu.VMEM((tokens, w.shape[0]), bf16),
-            dma((3,)), dma((2,)), dma((3,)), dma((3,)), dma((deep, 3)), dma((deep, 3)),
+            dma((3,)), dma((3,)), dma((3,)), dma((deep, 3)), dma((deep, 3)),
             dma((deep, 2)), dma((deep, 2)), dma((deep, 2)), dma((deep, 2)), dma, dma,
         ],
         compiler_params=pltpu.CompilerParams(collective_id=0, has_side_effects=True),

time: 29.8 us -> 27.3 us (0.916)
  Pallas kernels: 26.4 us -> 25.1 us
  local copies, waits for them, and re-layouts: 2.58 us -> 1.45 us
    pallas_call x1, Pallas kernels: 26.4 us -> 25.1 us  [kernel_shards(): pl.pallas_call(functools.partial(kernel, deep), out_shape=(pltpu.VMEM((to...]
    unnamed x4 -> x2, local copies, waits for them, and re-layouts: 2.58 us -> 1.45 us
where the time goes in v3:
time: 27.3 us; the launch traced here: 27.2 us
  Pallas kernels  25.1 us (92%)
  local copies, waits for them, and re-layouts  1.45 us (5%)
  between operations  0.64 us (2%)
    pallas_call x1, Pallas kernels, kernel_shards(): pl.pallas_call(functools.partial(kernel, deep), out_shape=(pltpu.VMEM((to...  25.1 us
    unnamed x2, local copies, waits for them, and re-layouts  1.45 us

profile of v3, /device:TPU:0, one launch (start us, length us, event | category | flops | bytes accessed | tf_op | source)
XLA Modules:
  0.0 27.2 jit_solution(10229647971946853585)
XLA Ops:
  0.6 25.1 %shard_map.68 = (bf16[128,2048]{1,0:T(8,128)(2,1)S(1)}, f32[64,512]{1,0:T(8,128)S(1)}) custom-call(s32[16]{0:T(128)} %mask_ref.1, s32[16]{0:T(128)} %list_ref.1, bf16[128,2048]{1,0:T(8,128)(2,1)} %x_hbm.1, bf16[128,512]{1,0:T(8,128)(2,1)} %s_hbm.1, bf16[1024,512]{1,0:T(8,128)(2,1)} %w_hbm.1), custom_call_target="tpu_custom_call" | custom-call | tf_op jit(solution)/shard_map/pallas_call | solution.py:263
  25.7 0.8 %copy.9 = bf16[128,2048]{1,0:T(8,128)(2,1)} copy(bf16[128,2048]{1,0:T(8,128)(2,1)S(1)} %get-tuple-element.2) | data formatting | bytes 1048576
  26.5 0.7 %copy.10 = f32[64,512]{1,0:T(8,128)} copy(f32[64,512]{1,0:T(8,128)S(1)} %get-tuple-element.3) | data formatting | bytes 262144

commit v4 on v3

--- a/solution.py
+++ b/solution.py
@@ -10,6 +10,7 @@
 MESH = pl.DeviceIdType.MESH
 CORES = 2
 WIDE = 2
+LAG = 2
 STEPS = 32766.0
 TINY = 1e-33
 
@@ -127,8 +128,6 @@
                 start = (xx * CORES * 2 + cy) * rows
                 tx[k, cy, xx * rows:(xx + 1) * rows, :] = part[start:start + rows, :]
 
-    load_x.wait()
-    turn(order[0])
     load_s.wait()
     pl.semaphore_wait(barrier, len(partners))
 
@@ -137,11 +136,11 @@
     s_fwd = remote(s_v.at[from_y], s_v.at[from_y], s_send_sem.at[2], s_recv_sem.at[2], sibling)
     s_y.start()
     s_sib.start()
+    load_x.wait()
 
     x_copies = {}
     for n, k in enumerate(order):
-        if n:
-            turn(k)
+        turn(k)
         copies = []
         for slot, (device, there) in enumerate(
             ((y_peer, from_y), (y_cross, from_cross), (sibling, from_sib))
@@ -231,9 +230,10 @@
     for n, k in enumerate(order):
         partial(k)
         send_x(k)
-        if n:
-            gather_x(order[n - 1])
-    gather_x(order[-1])
+        if n >= LAG:
+            gather_x(order[n - LAG])
+    for k in order[max(deep - LAG, 0):]:
+        gather_x(k)
 
     total = q[...]
     for k in range(1, deep):

time: 27.3 us -> 27.4 us (level)
  no operation moved by 1% of the time
where the time goes in v4:
time: 27.4 us; the launch traced here: 27.3 us
  Pallas kernels  25.2 us (92%)
  local copies, waits for them, and re-layouts  1.45 us (5%)
  between operations  0.64 us (2%)
    pallas_call x1, Pallas kernels, kernel_shards(): pl.pallas_call(functools.partial(kernel, deep), out_shape=(pltpu.VMEM((to...  25.2 us
    unnamed x2, local copies, waits for them, and re-layouts  1.45 us

profile of v4, /device:TPU:0, one launch (start us, length us, event | category | flops | bytes accessed | tf_op | source)
XLA Modules:
  0.0 27.3 jit_solution(14955586816109288009)
XLA Ops:
  0.6 25.2 %shard_map.68 = (bf16[128,2048]{1,0:T(8,128)(2,1)S(1)}, f32[64,512]{1,0:T(8,128)S(1)}) custom-call(s32[16]{0:T(128)} %mask_ref.1, s32[16]{0:T(128)} %list_ref.1, bf16[128,2048]{1,0:T(8,128)(2,1)} %x_hbm.1, bf16[128,512]{1,0:T(8,128)(2,1)} %s_hbm.1, bf16[1024,512]{1,0:T(8,128)(2,1)} %w_hbm.1), custom_call_target="tpu_custom_call" | custom-call | tf_op jit(solution)/shard_map/pallas_call | solution.py:263
  25.8 0.8 %copy.9 = bf16[128,2048]{1,0:T(8,128)(2,1)} copy(bf16[128,2048]{1,0:T(8,128)(2,1)S(1)} %get-tuple-element.2) | data formatting | bytes 1048576
  26.6 0.7 %copy.10 = f32[64,512]{1,0:T(8,128)} copy(f32[64,512]{1,0:T(8,128)S(1)} %get-tuple-element.3) | data formatting | bytes 262144
